TPU v7x, 1024 devices: a whole 4x4x32 slice. The times are simulated.
1024 devices in a mesh: grid: 64 (over x, z_hi, y), band: 16 (over z_lo, core).
Axes of the slice: x: 4, y: 4, z: 32 (z_hi: 4, z_lo: 8; z = z_hi * 8 + z_lo), core: 2. Of those that a mesh axis runs over, the one named last changes fastest.
Arguments:
- orbitals: bfloat16 [128, 64, 64, 128], P('band', 'grid'), may hold values from -6 to 6
- occupation: int32 [128], P('band'), may hold values from 1 to 2
- spin_of_band: int32 [128], P('band'), may hold values from 0 to 1
- ionic_charge: float32 [64, 64, 128], P('grid'), may hold values from 0.3 to 3
Outputs:
- potential: float32 [2, 64, 64, 128], P(None, 'grid')
- applied: bfloat16 [128, 64, 64, 128], P('band', 'grid')
All inputs are finite; a program needn't handle non-finite values.
Results may differ from a plain program's by a relative error of at most 0.001.
Values sent between devices are 32-bit elements; how exact they have to be, the bound alone decides.
A program may use at most 32 MiB of HBM per device.

v0:
```python
import math

import jax
import jax.numpy as jnp
from jax import lax
from jax.sharding import PartitionSpec as P

NZ = 64


spacing = 0.25
highest = lax.Precision.HIGHEST


def split_up(x, dim, peers):
    before, after = (x.shape[:dim], x.shape[dim + 1 :])
    return jnp.moveaxis(x.reshape(*before, peers, -1, *after), dim, 0)


def sum_at_owner(x, axis, dim):
    peers = lax.axis_size(axis)
    tiles = lax.all_to_all(split_up(x, dim, peers), axis, 0, 0, tiled=True)
    return jnp.sum(tiles, axis=0)


def sent_to_all(x, axis):
    peers = lax.axis_size(axis)
    return lax.all_to_all(jnp.broadcast_to(x[None], (peers, *x.shape)), axis, 0, 0, tiled=True)


def joined_along(tiles, dim):
    dims = list(tiles.shape[1:])
    dims[dim] *= tiles.shape[0]
    return jnp.moveaxis(tiles, 0, dim).reshape(dims)


def gather_directly(x, axis, dim):
    tiles = sent_to_all(x, axis)
    return joined_along(tiles, dim)


def tables(count):
    index = jnp.arange(count, dtype=jnp.int32)
    product = index[:, None] * index[None, :] % count
    angle = 2.0 * math.pi * product.astype(jnp.float32) / count
    return (jnp.cos(angle), jnp.sin(angle))


def signed_sq(index, count):
    signed = jnp.where(index < count // 2, index, index - count).astype(jnp.float32)
    wave = 2.0 * math.pi * signed / (count * spacing)
    return wave * wave


def kernel_at(depth, row_index, rows, col_index, cols):
    g_sq = signed_sq(jnp.arange(depth, dtype=jnp.int32), depth)[:, None, None]
    g_sq = g_sq + signed_sq(row_index, rows)[None, :, None]
    g_sq = g_sq + signed_sq(col_index, cols)[None, None, :]
    return jnp.where(g_sq > 0, 4.0 * math.pi / jnp.where(g_sq > 0, g_sq, 1.0), 0.0)


def along(table, field, form):
    return jnp.einsum(form, table, field, precision=highest)


def forward_y(cos_y, sin_y, real_x, imag_x):
    form_y = "ky,zyx->zkx"
    real_y = along(cos_y, real_x, form_y) + along(sin_y, imag_x, form_y)
    imag_y = along(cos_y, imag_x, form_y) - along(sin_y, real_x, form_y)
    return (real_y, imag_y)


def inverse_y(cos_y, sin_y, real_k, imag_k):
    form_y = "ky,zyx->zkx"
    plane_real = along(cos_y, real_k, form_y) - along(sin_y, imag_k, form_y)
    plane_imag = along(cos_y, imag_k, form_y) + along(sin_y, real_k, form_y)
    return (plane_real, plane_imag)


def z_kernel(cos_z, sin_z, moved, kernel):
    form_z = "kz,zyx->kyx"
    real_z = along(cos_z, moved[0], form_z) + along(sin_z, moved[1], form_z)
    imag_z = along(cos_z, moved[1], form_z) - along(sin_z, moved[0], form_z)
    real_k = real_z * kernel
    imag_k = imag_z * kernel
    back_real = along(cos_z, real_k, form_z) - along(sin_z, imag_k, form_z)
    back_imag = along(cos_z, imag_k, form_z) + along(sin_z, real_k, form_z)
    return jnp.stack([back_real, back_imag])


def solve_hartree(net, depth):
    planes, rows, cols = net.shape
    cos_x, sin_x = tables(cols)
    cos_y, sin_y = tables(rows)
    cos_z, sin_z = tables(depth)
    local_rows = rows // lax.axis_size("grid")
    row_index = lax.axis_index("grid") * local_rows + jnp.arange(local_rows, dtype=jnp.int32)
    real_x = jnp.dot(net, cos_x, precision=highest)
    imag_x = -jnp.dot(net, sin_x, precision=highest)
    real_y, imag_y = forward_y(cos_y, sin_y, real_x, imag_x)
    moved = lax.all_to_all(
        jnp.stack([real_y, imag_y]), "grid", split_axis=2, concat_axis=1, tiled=True
    )
    kernel = kernel_at(depth, row_index, rows, jnp.arange(cols, dtype=jnp.int32), cols)
    back = z_kernel(cos_z, sin_z, moved, kernel)
    returned = lax.all_to_all(back, "grid", split_axis=1, concat_axis=2, tiled=True)
    plane_real, plane_imag = inverse_y(cos_y, sin_y, returned[0], returned[1])
    result = jnp.dot(plane_real, cos_x, precision=highest) - jnp.dot(
        plane_imag, sin_x, precision=highest
    )
    return result / (cols * rows * depth)


def local(orbitals, occupation, spin_of_band, ionic_charge):
    bands, planes, rows, cols = orbitals.shape
    total = bands * lax.axis_size("band")
    channels = jnp.arange(2, dtype=jnp.int32)
    weights = (
        jnp.where(
            spin_of_band[None, :] == channels[:, None], occupation[None, :].astype(jnp.float32), 0.0
        )
        / total
    )
    values = orbitals.astype(jnp.float32)
    squares = (values * values).reshape(bands, -1)
    partial_value = jnp.dot(weights, squares, precision=highest).reshape(2, planes, rows, cols)
    share = sum_at_owner(partial_value, "band", 2)
    share_rows = share.shape[2]
    ion_share = lax.dynamic_slice_in_dim(
        ionic_charge, lax.axis_index("band") * share_rows, share_rows, 1
    )
    fields = jnp.concatenate(
        [-jnp.cbrt(6.0 / math.pi * share), (share[0] + share[1] - ion_share)[None]], 0
    )
    whole = gather_directly(fields, "band", 2)
    potential = solve_hartree(whole[2], NZ)[None] + whole[:2]
    pick = (spin_of_band[:, None] == channels[None, :]).astype(jnp.float32)
    chosen = jnp.dot(pick, potential.reshape(2, -1), precision=highest).reshape(
        bands, planes, rows, cols
    )
    applied = (chosen * values).astype(jnp.bfloat16)
    return (potential, applied)


def solution(mesh):
    return jax.shard_map(
        local,
        mesh=mesh,
        in_specs=(P("band", "grid", None, None), P("band"), P("band"), P("grid", None, None)),
        out_specs=(P(None, "grid", None, None), P("band", "grid", None, None)),
        check_vma=False,
    )
```

profile of v0, /device:TPU:1, one launch (start us, length us, event | category | flops | bytes accessed | tf_op | source)
XLA Modules:
  0.0 139.3 jit_solution(43942148281398369)
XLA Ops:
  0.6 1.0 convert_multiply_fusion
  1.7 0.6 copy-done.1
  2.3 1.0 convolution_bitcast_fusion.1
  3.3 17.4 %all-to-all-start = ((f32[16,2,1,4,128]{4,1,3,2,0:T(2,128)}), f32[16,2,1,4,128]{4,1,3,2,0:T(2,128)S(1)}, u32[]{:S(2)}, u32[]{:S(2)}) async-start(f32[16,2,1,4,128]{4,1,3,2,0:T(2,128)} %convolution_bitcast_fusion.1), calls=%async_computation | async-start | bytes 131072 | tf_op jit(solution)/shard_map/all_to_all | solution.py:22
  20.7 10.1 %all-to-all-done = f32[16,2,1,4,128]{4,1,3,2,0:T(2,128)S(1)} async-done(((f32[16,2,1,4,128]{4,1,3,2,0:T(2,128)}), f32[16,2,1,4,128]{4,1,3,2,0:T(2,128)S(1)}, u32[]{:S(2)}, u32[]{:S(2)}) %all-to-all-start) | async-done | bytes 65568 | tf_op jit(solution)/shard_map/all_to_all | solution.py:22
  30.9 0.7 fusion.65
  31.6 15.1 %all_to_all.28 = f32[16,3,1,4,128]{4,3,1,2,0:T(4,128)S(1)} all-to-all(f32[16,3,1,4,128]{4,3,1,2,0:T(4,128)S(1)} %broadcast_in_dim.27), channel_id=1, replica_groups=mesh['grid'=64,'band'=16] {'band'}, dimensions={0} | all-to-all | bytes 196608 | tf_op jit(solution)/shard_map/all_to_all | solution.py:28
  46.7 0.4 convolution_negate_fusion
  47.2 0.4 fusion.29
  48.8 0.7 copy.24
  49.5 23.3 %all-to-all-start.2 = ((f32[2,1,64,128]{3,1,0,2:T(1,128)}), f32[2,1,64,128]{3,1,0,2:T(1,128)S(1)}, u32[]{:S(2)}, u32[]{:S(2)}) async-start(f32[2,1,64,128]{3,1,0,2:T(1,128)} %copy.24), calls=%async_computation.2 | async-start | bytes 131072 | tf_op jit(solution)/shard_map/all_to_all | solution.py:101
  72.8 25.4 %all-to-all-done.2 = f32[2,1,64,128]{3,1,0,2:T(1,128)S(1)} async-done(((f32[2,1,64,128]{3,1,0,2:T(1,128)}), f32[2,1,64,128]{3,1,0,2:T(1,128)S(1)}, u32[]{:S(2)}, u32[]{:S(2)}) %all-to-all-start.2) | async-done | bytes 65568 | tf_op jit(solution)/shard_map/all_to_all | solution.py:101
  98.9 0.3 fusion.7
  99.5 0.3 fusion.8
  100.1 0.3 fusion.5
  100.4 0.3 fusion.6
  100.7 0.7 copy.25
  101.4 7.5 %all-to-all-start.3 = ((f32[2,64,1,128]{3,2,0,1:T(1,128)}), f32[2,64,1,128]{3,2,0,1:T(1,128)S(1)}, u32[]{:S(2)}, u32[]{:S(2)}) async-start(f32[2,64,1,128]{3,2,0,1:T(1,128)} %copy.25), calls=%async_computation.3 | async-start | bytes 131072 | tf_op jit(solution)/shard_map/all_to_all | solution.py:106
  109.0 26.2 %all-to-all-done.3 = f32[2,64,1,128]{3,2,0,1:T(1,128)S(1)} async-done(((f32[2,64,1,128]{3,2,0,1:T(1,128)}), f32[2,64,1,128]{3,2,0,1:T(1,128)S(1)}, u32[]{:S(2)}, u32[]{:S(2)}) %all-to-all-start.3) | async-done | bytes 65568 | tf_op jit(solution)/shard_map/all_to_all | solution.py:106
  136.1 0.4 fusion.27
  136.9 0.4 fusion.2
  137.3 0.6 add_bitcast_fusion
  138.3 0.3 fusion.1
  138.6 0.7 copy.30
  (33 shorter events, 4.1 us)
Async XLA Ops:
  0.6 1.0 copy-start.2
  1.7 0.7 copy-start.1
  3.3 27.5 %all-to-all-start = ((f32[16,2,1,4,128]{4,1,3,2,0:T(2,128)}), f32[16,2,1,4,128]{4,1,3,2,0:T(2,128)S(1)}, u32[]{:S(2)}, u32[]{:S(2)}) async-start(f32[16,2,1,4,128]{4,1,3,2,0:T(2,128)} %convolution_bitcast_fusion.1), calls=%async_computation | async-start | bytes 131072 | tf_op jit(solution)/shard_map/all_to_all | solution.py:22
  49.5 48.7 %all-to-all-start.2 = ((f32[2,1,64,128]{3,1,0,2:T(1,128)}), f32[2,1,64,128]{3,1,0,2:T(1,128)S(1)}, u32[]{:S(2)}, u32[]{:S(2)}) async-start(f32[2,1,64,128]{3,1,0,2:T(1,128)} %copy.24), calls=%async_computation.2 | async-start | bytes 131072 | tf_op jit(solution)/shard_map/all_to_all | solution.py:101
  101.4 33.8 %all-to-all-start.3 = ((f32[2,64,1,128]{3,2,0,1:T(1,128)}), f32[2,64,1,128]{3,2,0,1:T(1,128)S(1)}, u32[]{:S(2)}, u32[]{:S(2)}) async-start(f32[2,64,1,128]{3,2,0,1:T(1,128)} %copy.25), calls=%async_computation.3 | async-start | bytes 131072 | tf_op jit(solution)/shard_map/all_to_all | solution.py:106
  137.3 0.9 copy-start
where the time goes:
time: 141 us; the launch traced here: 139 us
  waiting for transfers between devices  61.7 us (44%)
  starting transfers between devices  48.2 us (34%)
  blocking collectives  15.1 us (11%)
  matrix products  7.76 us (6%)
  local copies, waits for them, and re-layouts  3.2 us (2%)
  other arithmetic  2.43 us (2%)
    all_to_all x1, waiting for transfers between devices, solve_hartree(): lax.all_to_all(back, 'grid', split_axis=1, concat_axis=2, tiled=True)  26.2 us
    all_to_all x1, waiting for transfers between devices, solve_hartree(): lax.all_to_all(jnp.stack([real_y, imag_y]), 'grid', split_axis=2, concat_...  25.4 us
    all_to_all x1, starting transfers between devices, solve_hartree(): lax.all_to_all(jnp.stack([real_y, imag_y]), 'grid', split_axis=2, concat_...  23.3 us
    all_to_all x1, starting transfers between devices, sum_at_owner(): tiles = lax.all_to_all(split_up(x, dim, peers), axis, 0, 0, tiled=True)  17.4 us
    all_to_all x1, blocking collectives, sent_to_all(): lax.all_to_all(jnp.broadcast_to(x[None], (peers, *x.shape)), axis, 0, 0,...  15.1 us
    all_to_all x1, waiting for transfers between devices, sum_at_owner(): tiles = lax.all_to_all(split_up(x, dim, peers), axis, 0, 0, tiled=True)  10.1 us
    all_to_all x1, starting transfers between devices, solve_hartree(): lax.all_to_all(back, 'grid', split_axis=1, concat_axis=2, tiled=True)  7.47 us
    dot_general x16, matrix products, along(): return jnp.einsum(form, table, field, precision=highest)  4.7 us
  transfers between devices with their start and end apart: 3, of which 3 were waited for; matrix products, arithmetic and copies ran while one was open for 0% of the time, Pallas kernels for 0%

commit v1 on v0

v1 whole, which is shorter than its diff:
```python
import functools
import math

import jax
import jax.numpy as jnp
import numpy as np
from jax import lax
from jax.experimental import pallas as pl
from jax.experimental.pallas import tpu as pltpu
from jax.sharding import PartitionSpec as P

X, H, Y, L = 4, 4, 4, 8
SPACING = 0.25
MESH = pl.DeviceIdType.MESH
HIGHEST = lax.Precision.HIGHEST


def cas(count):
    index = np.arange(count)
    angle = 2.0 * np.pi * ((index[:, None] * index[None, :]) % count) / count
    return (np.cos(angle) + np.sin(angle)).astype(np.float32)


def wave_sq(count):
    index = np.arange(count)
    signed = np.where(index < count // 2, index, index - count)
    return (2.0 * np.pi * signed / (count * SPACING)) ** 2


def green(depth, rows, cols):
    g_sq = wave_sq(depth)[:, None, None] + wave_sq(rows)[None, :, None] + wave_sq(cols)[None, None, :]
    kernel = np.where(g_sq > 0, 4.0 * np.pi / np.where(g_sq > 0, g_sq, 1.0), 0.0)
    index = np.arange(depth)
    cos_z = np.cos(2.0 * np.pi * ((index[:, None] * index[None, :]) % depth) / depth)
    table = np.tensordot(cos_z, kernel, 1) / (depth * rows * cols)
    share = rows // L
    return np.ascontiguousarray(
        table.reshape(depth, L, share, cols).transpose(1, 0, 2, 3).astype(np.float32)
    )


def dot(a, b):
    return jnp.dot(a, b, precision=HIGHEST, preferred_element_type=jnp.float32)


def wrap(value, count):
    return lax.rem(value + count, count)


def field_kernel(
    total,
    occ, spin, orb_hbm, ion_hbm, hx_hbm, hy_hbm, g_hbm,
    out,
    orb, ion, hx, hy, gz,
    d_own, t_own, t_in, d_in,
    spec, ra, pb, rb, cs, rc, vb, rd, hart, ex_in,
    ds, rr, es, ex, h_in,
    load_sem, send, recv,
):
    rows = hy.shape[0]
    share = rows // L
    ring = H * L
    half = L // 2
    depth = X * H * Y
    g, b = lax.axis_index("grid"), lax.axis_index("band")
    x, h, y = lax.div(g, H * Y), lax.rem(lax.div(g, Y), H), lax.rem(g, Y)
    l, c = lax.div(b, 2), lax.rem(b, 2)
    p = h * L + l
    side = 2 * lax.div(l, half) - 1

    def at(dx, dy, place, core):
        row = (wrap(x + dx, X) * H + lax.div(place, L)) * Y + wrap(y + dy, Y)
        return (row, lax.rem(place, L) * 2 + core)

    partner = (g, b + 1 - 2 * c)
    window = [o for o in range(-half, half + 1) if o != 0]
    inward = [o for o in range(-half, half) if o != 0]
    others = [(dx, dy) for dx in range(X) for dy in range(Y) if dx + dy > 0]

    loads = [
        pltpu.make_async_copy(src, dst, load_sem.at[i])
        for i, (src, dst) in enumerate(
            [(orb_hbm, orb), (ion_hbm, ion), (hx_hbm, hx), (hy_hbm, hy), (g_hbm.at[l], gz)]
        )
    ]
    for load in loads:
        load.start()

    barrier = pltpu.get_barrier_semaphore()

    def greet(device):
        pl.semaphore_signal(barrier, inc=1, device_id=device, device_id_type=MESH)

    greet(partner)

    @pl.when(c == 1)
    def _():
        for o in window:
            greet(at(0, 0, wrap(p + o, ring), 1))
        for j in range(1, H):
            greet(at(0, 0, wrap(p + j * L, ring), 1))
        for dx, dy in others:
            greet(at(dx, dy, p, 1))

    @pl.when(c == 0)
    def _():
        for j in range(1, L):
            greet(at(0, 0, h * L + lax.rem(l + j, L), 0))

    loads[0].wait()
    w = [occ[i].astype(jnp.float32) / total for i in range(orb.shape[0])]
    up = [spin[i].astype(jnp.float32) for i in range(orb.shape[0])]
    d0 = jnp.zeros(t_own.shape, jnp.float32)
    d1 = jnp.zeros(t_own.shape, jnp.float32)
    for i in range(orb.shape[0]):
        value = orb[i].astype(jnp.float32)
        square = value * value
        d0 = d0 + (w[i] * (1.0 - up[i])) * square
        d1 = d1 + (w[i] * up[i]) * square
    d_own[0] = d0
    d_own[1] = d1
    t_own[...] = d0 + d1

    for load in loads[1:]:
        load.wait()

    def remote(src, dst, phase, device):
        return pltpu.make_async_remote_copy(
            src_ref=src, dst_ref=dst, send_sem=send.at[phase], recv_sem=recv.at[phase],
            device_id=device, device_id_type=MESH,
        )

    def arrived(like, phase):
        remote(like, like, phase, partner).wait_recv()

    def sent(like, phase):
        remote(like, like, phase, partner).wait_send()

    @pl.when(c == 1)
    def _():
        pl.semaphore_wait(barrier, 1 + len(window) + H - 1 + len(others))
        remote(d_own, d_in, 0, partner).start()
        arrived(t_in, 1)
        charge = t_own[...] + t_in[...] - ion[...] * (1.0 / L)
        spec[...] = dot(dot(hy[...], charge), hx[...])
        for o in sorted(inward, key=abs, reverse=True):
            place = wrap(p - o, ring)
            rows_of = pl.ds(pl.multiple_of(lax.rem(place, L) * share, share), share)
            remote(spec.at[rows_of], ra.at[inward.index(o)], 2, at(0, 0, place, 1)).start()
        own = spec[pl.ds(pl.multiple_of(l * share, share), share), :]
        arrived(ra, 2)
        other = jnp.zeros_like(own)
        for slot, o in enumerate(inward):
            block = ra[slot]
            mine = lax.div(wrap(p + o, ring), L) == h
            own = own + jnp.where(mine, block, 0.0)
            other = other + jnp.where(mine, 0.0, block)
        pb[0] = own
        pb[1] = other
        for j in sorted(range(1, H), key=lambda j: -min(j, H - j)):
            remote(pb, rb.at[j - 1], 3, at(0, 0, wrap(p + j * L, ring), 1)).start()
        arrived(rb, 3)
        first = [pb[0]] + [rb[j - 1, 0] for j in range(1, H)]
        second = [pb[1]] + [rb[j - 1, 1] for j in range(1, H)]
        left = side < 0
        planes = [
            first[j] + jnp.where(left, second[(j - 1) % H], second[(j + 1) % H]) for j in range(H)
        ]

        def response(dx, dy, t):
            tx, ty, th = wrap(x + dx, X), wrap(y + dy, Y), wrap(h + t * side, H)
            target = (tx * H + th) * Y + ty
            value = None
            for j in range(H):
                source = (x * H + wrap(h - j, H)) * Y + y
                term = gz[wrap(target - source, depth)] * planes[j]
                value = term if value is None else value + term
            return value

        hops = lambda d: min(d[0], X - d[0]) + min(d[1], Y - d[1])
        for dx, dy in sorted(others, key=hops, reverse=True):
            slot = others.index((dx, dy))
            for t in range(2):
                cs[slot, t] = response(dx, dy, t)
            remote(cs.at[slot], rc.at[slot], 4, at(dx, dy, p, 1)).start()
        now = [response(0, 0, t) for t in range(2)]
        arrived(rc, 4)
        for slot in range(len(others)):
            now = [now[t] + rc[slot, t] for t in range(2)]
        vb[0] = now[0]
        vb[1] = now[1]
        mine_rows = pl.ds(pl.multiple_of(l * share, share), share)
        rd[mine_rows, :] = now[0]
        for o in sorted(inward, key=abs, reverse=True):
            place = wrap(p + o, ring)
            plane = lax.div(place, L)
            differs = (plane != h).astype(jnp.int32)
            remote(vb.at[differs], rd.at[mine_rows], 5, at(0, 0, place, 1)).start()
        arrived(rd.at[pl.ds(0, rows - share)], 5)
        hart[...] = dot(dot(hy[...], rd[...]), hx[...])
        remote(hart, h_in, 6, partner).start()
        arrived(ex_in, 7)
        out[0] = hart[...] + ex_in[0]
        out[1] = hart[...] + ex_in[1]
        sent(d_own, 0)
        sent(ra, 2)
        sent(rb, 3)
        sent(rc, 4)
        sent(rd.at[pl.ds(0, rows - share)], 5)
        sent(hart, 6)

    @pl.when(c == 0)
    def _():
        pl.semaphore_wait(barrier, L)
        remote(t_own, t_in, 1, partner).start()
        arrived(d_in, 0)
        ds[...] = d_own[...] + d_in[...]
        for j in range(1, L):
            to = lax.rem(l + j, L)
            rows_of = pl.ds(pl.multiple_of(to * share, share), share)
            remote(ds.at[:, rows_of, :], rr.at[j - 1], 2, at(0, 0, h * L + to, 0)).start()
        mine_rows = pl.ds(pl.multiple_of(l * share, share), share)
        density = ds[:, mine_rows, :]
        arrived(rr, 2)
        for j in range(L - 1):
            density = density + rr[j]
        scaled = (6.0 / math.pi) * density
        positive = scaled > 0.0
        root = jnp.exp(jnp.log(jnp.where(positive, scaled, 1.0)) * (1.0 / 3.0))
        es[...] = jnp.where(positive, -root, 0.0)
        ex[:, mine_rows, :] = es[...]
        for j in range(1, L):
            to = lax.rem(l + j, L)
            remote(es, ex.at[:, mine_rows, :], 3, at(0, 0, h * L + to, 0)).start()
        arrived(rr, 3)
        remote(ex, ex_in, 7, partner).start()
        arrived(h_in, 6)
        out[0] = h_in[...] + ex[0]
        out[1] = h_in[...] + ex[1]
        sent(t_own, 1)
        sent(rr, 2)
        sent(rr, 3)
        sent(ex, 7)


def apply_kernel(spin, pot, orb, potential, applied):
    potential[...] = pot[...]
    for i in range(orb.shape[0]):
        chosen = jnp.where(spin[i] == 1, pot[1], pot[0])
        applied[i] = (chosen * orb[i].astype(jnp.float32)).astype(jnp.bfloat16)


def local(orbitals, occupation, spin_of_band, ionic_charge):
    bands, planes, rows, cols = orbitals.shape
    depth = X * H * Y
    share = rows // L
    total = bands * lax.axis_size("band")
    orb = orbitals.reshape(bands, rows, cols)
    f32 = jnp.float32
    plane, pair = (rows, cols), (2, rows, cols)
    vmem = lambda *shape: pltpu.VMEM(shape, f32)
    others = X * Y - 1
    hbm = pl.BlockSpec(memory_space=pl.ANY)
    smem = pl.BlockSpec(memory_space=pltpu.SMEM)
    invmem = pl.BlockSpec(memory_space=pltpu.VMEM)
    pot = pl.pallas_call(
        functools.partial(field_kernel, float(total)),
        out_shape=jax.ShapeDtypeStruct(pair, f32),
        in_specs=[smem, smem, hbm, hbm, hbm, hbm, hbm],
        out_specs=invmem,
        scratch_shapes=[
            pltpu.VMEM((bands, rows, cols), jnp.bfloat16),
            vmem(*plane), vmem(cols, cols), vmem(rows, rows), vmem(depth, share, cols),
            vmem(*pair), vmem(*plane), vmem(*plane), vmem(*pair),
            vmem(*plane), vmem(L - 1, share, cols), vmem(2, share, cols),
            vmem(H - 1, 2, share, cols), vmem(others, 2, share, cols), vmem(others, 2, share, cols),
            vmem(2, share, cols), vmem(*plane), vmem(*plane), vmem(*pair),
            vmem(*pair), vmem(L - 1, 2, share, cols), vmem(2, share, cols), vmem(*pair), vmem(*plane),
            pltpu.SemaphoreType.DMA((5,)),
            pltpu.SemaphoreType.DMA((8,)),
            pltpu.SemaphoreType.DMA((8,)),
        ],
        compiler_params=pltpu.CompilerParams(collective_id=0, has_side_effects=True),
        name="field",
    )(
        occupation, spin_of_band, orb, ionic_charge.reshape(rows, cols),
        jnp.asarray(cas(cols)), jnp.asarray(cas(rows)), jnp.asarray(green(depth, rows, cols)),
    )
    potential, applied = pl.pallas_call(
        apply_kernel,
        out_shape=(
            jax.ShapeDtypeStruct(pair, f32),
            jax.ShapeDtypeStruct((bands, rows, cols), jnp.bfloat16),
        ),
        in_specs=[smem, invmem, invmem],
        out_specs=(invmem, invmem),
        name="apply",
    )(spin_of_band, pot, orb)
    return (
        potential.reshape(2, planes, rows, cols),
        applied.reshape(bands, planes, rows, cols),
    )


def solution(mesh):
    return jax.shard_map(
        local,
        mesh=mesh,
        in_specs=(P("band", "grid", None, None), P("band"), P("band"), P("grid", None, None)),
        out_specs=(P(None, "grid", None, None), P("band", "grid", None, None)),
        check_vma=False,
    )
```

time: 141 us -> 57.3 us (0.41); the launches traced: 139 us -> 57.1 us
  waiting for transfers between devices: 61.7 us -> 0 us
  Pallas kernels: 0 us -> 56.5 us
  starting transfers between devices: 48.2 us -> 0 us
  blocking collectives: 15.1 us -> 0 us
  matrix products: 7.76 us -> 0 us
  local copies, waits for them, and re-layouts: 3.2 us -> 0 us
  other arithmetic: 2.43 us -> 0 us
    all_to_all x3 -> x0, waiting for transfers between devices: 61.7 us -> none  [the longest x1 26.2 us: solve_hartree(): lax.all_to_all(back, 'grid', split_axis=1, concat_axis=2, tiled=True)]
    pallas_call x0 -> x2, Pallas kernels: none -> 56.5 us  [the longest x1 54.8 us: local(): pl.pallas_call(functools.partial(field_kernel, float(total)), out_shape=j...]
    all_to_all x3 -> x0, starting transfers between devices: 48.2 us -> none  [the longest x1 23.3 us: solve_hartree(): lax.all_to_all(jnp.stack([real_y, imag_y]), 'grid', split_axis=2, concat_...]
    all_to_all x1 -> x0, blocking collectives: 15.1 us -> none  [sent_to_all(): lax.all_to_all(jnp.broadcast_to(x[None], (peers, *x.shape)), axis, 0, 0,...]
    dot_general x22 -> x0, matrix products: 7.76 us -> none  [the longest x16 4.7 us: along(): return jnp.einsum(form, table, field, precision=highest)]
    unnamed x7 -> x0, local copies, waits for them, and re-layouts: 1.62 us -> none
  transfers between devices with their start and end apart: 3 -> 0, of which waited for: 3 -> 0; matrix products, arithmetic and copies ran while one was open for 0% -> 0% of each run, Pallas kernels for 0% -> 0%
where the time goes in v1:
time: 57.3 us; the launch traced here: 57.1 us
  Pallas kernels  56.5 us (99%)
  between operations  0.64 us (1%)
    pallas_call x1, Pallas kernels, local(): pl.pallas_call(functools.partial(field_kernel, float(total)), out_shape=j...  54.8 us
    pallas_call x1, Pallas kernels, local(): pl.pallas_call(apply_kernel, out_shape=(jax.ShapeDtypeStruct(pair, f32),...  1.65 us

profile of v1, /device:TPU:1, one launch (start us, length us, event | category | flops | bytes accessed | tf_op | source)
XLA Modules:
  0.0 57.1 jit_solution(11782456227704853729)
XLA Ops:
  0.6 54.8 %field.1.pot = f32[2,64,128]{2,1,0:T(8,128)} custom-call(s32[8]{0:T(128)} %occ.1, s32[8]{0:T(128)} %spin.3, bf16[8,64,128]{2,1,0:T(8,128)(2,1)} %bitcast.8, f32[64,128]{1,0:T(8,128)} %bitcast.10, f32[128,128]{1,0:T(8,128)} %constant.6.clone.hx_hbm, f32[64,64]{1,0:T(8,128)} %constant.7.clone.hy_hbm, f32[8,64,8,128]{3,2,1,0:T(8,128)} %constant.8.clone.g_hbm), custom_call_target="tpu_custom_call" | custom-call | tf_op jit(solution)/shard_map/field/pallas_call | solution.py:266
  55.4 1.6 %apply.1 = (f32[2,64,128]{2,1,0:T(8,128)}, bf16[8,64,128]{2,1,0:T(8,128)(2,1)}) custom-call(s32[8]{0:T(128)} %spin.3, f32[2,64,128]{2,1,0:T(8,128)} %field.1.pot, bf16[8,64,128]{2,1,0:T(8,128)(2,1)} %bitcast.9), custom_call_target="tpu_custom_call" | custom-call | tf_op jit(solution)/shard_map/apply/pallas_call | solution.py:289
